TPU v7x, 128 devices: a whole 4x4x4 slice. The times are simulated.
128 devices in a mesh: grp: 4 (over y), row: 32 (over z, x, core).
Axes of the slice: x: 4, y: 4, z: 4, core: 2. Of those that a mesh axis runs over, the one named last changes fastest.
Arguments:
- tiles: bfloat16 [4, 32, 32, 256, 256], P('grp', 'row'), may hold values from -0.046875 to 0.046875
- tile_rows: int32 [4, 32, 32], P('grp', 'row'), may hold values from 0 to 3, as said below
- tile_cols: int32 [4, 32, 32], P('grp', 'row'), may hold values from 0 to 31, as said below
- live_tiles: int32 [4, 32], P('grp', 'row'), may hold values from 16 to 32, as said below
- dual_shift: float32 [32768], P('row'), may hold values from 0.5 to 2
- start_block: float32 [32, 32768], P(None, 'row'), may hold values from -6 to 6
Outputs:
- projections: float32 [4, 32, 128], replicated
- factors: float32 [4, 32, 32], replicated
- next_block: float32 [32, 32768], P(None, 'row')
Inputs may be any that keep to these rules, and one draw needn't show every extreme that they name: `tile_rows`: the tile slots of one device sit at distinct positions (block row, column block), padding slots included. `tile_cols`: column block j of group g is global block column (j // 1) * 4 + g * 1 + j % 1. Slots from live_tiles on are padding with arbitrary values; in every draw some device has all 32 slots live.
All inputs are finite; a program needn't handle non-finite values.
Results may differ from a plain program's by a relative error of at most 0.013.
Values may be sent and summed in bfloat16 or wider, within the bound.
A program may use at most 64 MiB of HBM per device.

v0:
```python
import jax
import jax.numpy as jnp
from jax import lax
from jax.sharding import PartitionSpec as P

ITERS = 4


def in_order(parts, dim):
    parts = jnp.moveaxis(parts, 0, dim)
    lengths = parts.shape
    return parts.reshape(*lengths[:dim], lengths[dim] * lengths[dim + 1], *lengths[dim + 2 :])


def copy_for_each(value, axis):
    size = lax.axis_size(axis)
    return lax.all_to_all(
        jnp.broadcast_to(value[None], (size, *value.shape)), axis, 0, 0, tiled=True
    )


def gathered_copies(value, axis, dim):
    return in_order(copy_for_each(value, axis), dim)


def split_up(value, dim, size):
    before, after = (value.shape[:dim], value.shape[dim + 1 :])
    return jnp.moveaxis(value.reshape(*before, size, -1, *after), dim, 0)


def sent_and_summed(value, axis, dim):
    parts = split_up(value, dim, lax.axis_size(axis))
    arrived = lax.all_to_all(parts, axis, split_axis=0, concat_axis=0, tiled=True)
    return arrived.astype(jnp.float32).sum(axis=0)


def of_everyone(value, axis):
    return copy_for_each(value, axis).sum(axis=0)


def inner_product(left, right):
    return lax.dot_general(
        left,
        right,
        (((1,), (1,)), ((), ())),
        precision=lax.Precision.HIGHEST,
        preferred_element_type=jnp.float32,
    )


def apply_matrix(left, right):
    return jnp.dot(left, right, precision=lax.Precision.HIGHEST, preferred_element_type=jnp.float32)


def per_device(tiles, tile_rows, tile_cols, live_tiles, dual_shift, start_block):
    matrix = tiles[0, 0]
    rows_here = tile_rows[0, 0]
    cols_here = tile_cols[0, 0]
    tile_count = matrix.shape[0]
    tile_edge = matrix.shape[1]
    vec_width = start_block.shape[0]
    row_count = start_block.shape[1]
    group_count = lax.axis_size("grp")
    owner_count = lax.axis_size("row")
    owned_blocks = row_count // tile_edge
    quarter_tiles = owned_blocks // group_count
    column_tiles = quarter_tiles * owner_count
    group_index = lax.axis_index("grp")
    live_mask = (jnp.arange(tile_count) < live_tiles[0, 0]).astype(jnp.float32)
    row_table = (rows_here[:, None] == jnp.arange(owned_blocks)[None, :]).astype(
        jnp.float32
    ) * live_mask[:, None]
    col_table = (cols_here[:, None] == jnp.arange(column_tiles)[None, :]).astype(
        jnp.float32
    ) * live_mask[:, None]

    def partial_of(full_rows, group_rows):
        gathered = gathered_copies(group_rows, "row", 1)
        forward = jnp.einsum(
            "kbc,brc->kbr",
            jnp.take(gathered, cols_here, axis=1),
            matrix,
            preferred_element_type=jnp.float32,
        )
        direct = jnp.einsum("kbr,bi->kir", forward, row_table)
        backward = jnp.einsum(
            "kbr,brc->kbc",
            jnp.take(full_rows, rows_here, axis=1),
            matrix,
            preferred_element_type=jnp.float32,
        )
        spread = jnp.einsum("kbc,bj->kjc", backward, col_table)
        mine = sent_and_summed(spread.astype(jnp.bfloat16), "row", 1)
        placed = lax.dynamic_update_slice_in_dim(
            jnp.zeros_like(direct), mine, group_index * quarter_tiles, 1
        )
        return 0.5 * (direct + placed)

    def split_parts(vectors):
        rounded = vectors.astype(jnp.bfloat16).reshape(vec_width, owned_blocks, tile_edge)
        return (
            rounded,
            lax.dynamic_slice_in_dim(rounded, group_index * quarter_tiles, quarter_tiles, 1),
        )

    def finish_sum(partial_value):
        return of_everyone(partial_value, "grp").reshape(vec_width, row_count)

    def reduce_dots(values):
        return of_everyone(values, "row")

    def orthonormal(block, gram_matrix):
        lower_factor = jnp.linalg.cholesky(gram_matrix)
        return (
            lax.linalg.triangular_solve(lower_factor, block, left_side=True, lower=True),
            lower_factor,
        )

    current, unused = orthonormal(start_block, reduce_dots(inner_product(start_block, start_block)))
    total_cols = ITERS * vec_width
    basis_rows = jnp.zeros((total_cols, current.shape[1]), jnp.float32)
    projections = jnp.zeros((ITERS, vec_width, total_cols), jnp.float32)
    factors = jnp.zeros((ITERS, vec_width, vec_width), jnp.float32)

    def lanczos_step(step_index, state_now):
        current, basis_rows, projections, factors = state_now
        basis_rows = lax.dynamic_update_slice_in_dim(basis_rows, current, step_index * vec_width, 0)
        full_rows, group_rows = split_parts(current)
        image = finish_sum(partial_of(full_rows, group_rows)) - current * dual_shift[None, :]
        first_coef = reduce_dots(inner_product(image, basis_rows))
        image = image - apply_matrix(first_coef, basis_rows)
        gram_matrix = reduce_dots(inner_product(image, image))
        current, lower_factor = orthonormal(image, gram_matrix)
        projections = lax.dynamic_update_index_in_dim(projections, first_coef, step_index, 0)
        factors = lax.dynamic_update_index_in_dim(factors, lower_factor, step_index, 0)
        return (current, basis_rows, projections, factors)

    current, basis_rows, projections, factors = lax.fori_loop(
        0, ITERS, lanczos_step, (current, basis_rows, projections, factors)
    )
    return (projections, factors, current)


def solution(mesh):
    in_specs = (
        P("grp", "row", None, None, None),
        P("grp", "row", None),
        P("grp", "row", None),
        P("grp", "row"),
        P("row"),
        P(None, "row"),
    )
    out_specs = (P(), P(), P(None, "row"))
    return jax.shard_map(
        per_device, mesh=mesh, in_specs=in_specs, out_specs=out_specs, check_vma=False
    )
```

profile of v0, /device:TPU:1, one launch (start us, length us, event | category | flops | bytes accessed | tf_op | source)
XLA Modules:
  0.0 370.9 jit_solution(16995554148360917860)
XLA Ops:
  2.8 9.4 %all-to-all-start.5 = ((f32[32,1,1024]{2,1,0:T(1,128)}), f32[32,1,1024]{2,1,0:T(1,128)S(1)}, u32[]{:S(2)}, u32[]{:S(2)}) async-start(f32[32,1,1024]{2,1,0:T(1,128)} %reshape.192), calls=%async_computation.5 | async-start | bytes 262144 | tf_op jit(solution)/shard_map/all_to_all | solution.py:17
  12.9 6.9 %all-to-all-done.5 = f32[32,1,1024]{2,1,0:T(1,128)S(1)} async-done(((f32[32,1,1024]{2,1,0:T(1,128)}), f32[32,1,1024]{2,1,0:T(1,128)S(1)}, u32[]{:S(2)}, u32[]{:S(2)}) %all-to-all-start.5) | async-done | bytes 131104 | tf_op jit(solution)/shard_map/all_to_all | solution.py:17
  28.7 341.6 %while.23 = (s32[]{:T(128)}, f32[32,1024]{1,0:T(8,128)S(1)}, f32[128,1024]{1,0:T(8,128)S(1)}, f32[4,32,128]{2,1,0:T(8,128)}, f32[4,32,32]{2,1,0:T(8,128)}, /*ind...) while((s32[]{:T(128)}, f32[32,1024]{1,0:T(8,128)S(1)}, ...), condition=%wide.region_8.11_spmd.clone.clone, body=%wide.region_3.10_spmd.clone.clone.sunk | while | flops 414691168 | bytes 29908952 | solution.py:138
  29.7 3.9 %all-to-all-start = ((bf16[32,32,1,256]{3,1,2,0:T(8,128)(2,1)}), bf16[32,32,1,256]{3,1,2,0:T(8,128)(2,1)S(1)}, u32[]{:S(2)}, u32[]{:S(2)}) async-start(bf16[32,32,1,256]{3,1,2,0:T(8,128)(2,1)} %broadcast_in_dim.179), calls=%async_computation | async-start | bytes 1048576 | tf_op jit(solution)/shard_map/while/body/eval_jaxpr/all_to_all | solution.py:17
  40.2 5.0 %all-to-all-done = bf16[32,32,1,256]{3,1,2,0:T(8,128)(2,1)S(1)} async-done(((bf16[32,32,1,256]{3,1,2,0:T(8,128)(2,1)}), bf16[32,32,1,256]{3,1,2,0:T(8,128)(2,1)S(1)}, u32[]{:S(2)}, u32[]{:S(2)}) %all-to-all-start) | async-done | bytes 524320 | tf_op jit(solution)/shard_map/while/body/eval_jaxpr/all_to_all | solution.py:17
  45.2 3.9 %all-to-all-start.1 = ((bf16[32,32,1,256]{3,1,2,0:T(8,128)(2,1)}), bf16[32,32,1,256]{3,1,2,0:T(8,128)(2,1)S(1)}, u32[]{:S(2)}, u32[]{:S(2)}) async-start(bf16[32,32,1,256]{3,1,2,0:T(8,128)(2,1)} %copy.79), calls=%async_computation.1 | async-start | bytes 1048576 | tf_op jit(solution)/shard_map/while/body/eval_jaxpr/all_to_all | solution.py:33
  53.7 6.9 %all-to-all-done.1 = bf16[32,32,1,256]{3,1,2,0:T(8,128)(2,1)S(1)} async-done(((bf16[32,32,1,256]{3,1,2,0:T(8,128)(2,1)}), bf16[32,32,1,256]{3,1,2,0:T(8,128)(2,1)S(1)}, u32[]{:S(2)}, u32[]{:S(2)}) %all-to-all-start.1) | async-done | bytes 524320 | tf_op jit(solution)/shard_map/while/body/eval_jaxpr/all_to_all | solution.py:33
  60.8 12.6 %all_to_all.75 = f32[4,32,4,256]{3,1,2,0:T(8,128)S(1)} all-to-all(f32[4,32,4,256]{3,1,2,0:T(8,128)S(1)} %broadcast_in_dim.180), channel_id=1, replica_groups=mesh['grp'=4,'row'=32] {'grp'}, dimensions={0} | all-to-all | bytes 1048576 | tf_op jit(solution)/shard_map/while/body/eval_jaxpr/all_to_all | solution.py:17
  75.0 5.5 %all-to-all-start.3 = ((f32[32,32,128]{2,1,0:T(8,128)}), f32[32,32,128]{2,1,0:T(8,128)S(1)}, u32[]{:S(2)}, u32[]{:S(2)}) async-start(f32[32,32,128]{2,1,0:T(8,128)} %broadcast_in_dim.181), calls=%async_computation.3 | async-start | bytes 1048576 | tf_op jit(solution)/shard_map/while/body/eval_jaxpr/all_to_all | solution.py:17
  80.4 11.4 %all-to-all-done.3 = f32[32,32,128]{2,1,0:T(8,128)S(1)} async-done(((f32[32,32,128]{2,1,0:T(8,128)}), f32[32,32,128]{2,1,0:T(8,128)S(1)}, u32[]{:S(2)}, u32[]{:S(2)}) %all-to-all-start.3) | async-done | bytes 524320 | tf_op jit(solution)/shard_map/while/body/eval_jaxpr/all_to_all | solution.py:17
  98.1 7.1 %all-to-all-done.4 = f32[32,1,1024]{2,1,0:T(1,128)S(1)} async-done(((f32[32,1,1024]{2,1,0:T(1,128)}), f32[32,1,1024]{2,1,0:T(1,128)S(1)}, u32[]{:S(2)}, u32[]{:S(2)}) %all-to-all-start.4) | async-done | bytes 131104 | tf_op jit(solution)/shard_map/while/body/eval_jaxpr/all_to_all | solution.py:17
  116.3 3.9 %all-to-all-start = ((bf16[32,32,1,256]{3,1,2,0:T(8,128)(2,1)}), bf16[32,32,1,256]{3,1,2,0:T(8,128)(2,1)S(1)}, u32[]{:S(2)}, u32[]{:S(2)}) async-start(bf16[32,32,1,256]{3,1,2,0:T(8,128)(2,1)} %broadcast_in_dim.179), calls=%async_computation | async-start | bytes 1048576 | tf_op jit(solution)/shard_map/while/body/eval_jaxpr/all_to_all | solution.py:17
  126.8 5.0 %all-to-all-done = bf16[32,32,1,256]{3,1,2,0:T(8,128)(2,1)S(1)} async-done(((bf16[32,32,1,256]{3,1,2,0:T(8,128)(2,1)}), bf16[32,32,1,256]{3,1,2,0:T(8,128)(2,1)S(1)}, u32[]{:S(2)}, u32[]{:S(2)}) %all-to-all-start) | async-done | bytes 524320 | tf_op jit(solution)/shard_map/while/body/eval_jaxpr/all_to_all | solution.py:17
  140.3 6.9 %all-to-all-done.1 = bf16[32,32,1,256]{3,1,2,0:T(8,128)(2,1)S(1)} async-done(((bf16[32,32,1,256]{3,1,2,0:T(8,128)(2,1)}), bf16[32,32,1,256]{3,1,2,0:T(8,128)(2,1)S(1)}, u32[]{:S(2)}, u32[]{:S(2)}) %all-to-all-start.1) | async-done | bytes 524320 | tf_op jit(solution)/shard_map/while/body/eval_jaxpr/all_to_all | solution.py:33
  147.4 11.6 %all_to_all.75 = f32[4,32,4,256]{3,1,2,0:T(8,128)S(1)} all-to-all(f32[4,32,4,256]{3,1,2,0:T(8,128)S(1)} %broadcast_in_dim.180), channel_id=1, replica_groups=mesh['grp'=4,'row'=32] {'grp'}, dimensions={0} | all-to-all | bytes 1048576 | tf_op jit(solution)/shard_map/while/body/eval_jaxpr/all_to_all | solution.py:17
  160.5 4.8 %all-to-all-start.3 = ((f32[32,32,128]{2,1,0:T(8,128)}), f32[32,32,128]{2,1,0:T(8,128)S(1)}, u32[]{:S(2)}, u32[]{:S(2)}) async-start(f32[32,32,128]{2,1,0:T(8,128)} %broadcast_in_dim.181), calls=%async_computation.3 | async-start | bytes 1048576 | tf_op jit(solution)/shard_map/while/body/eval_jaxpr/all_to_all | solution.py:17
  165.3 11.5 %all-to-all-done.3 = f32[32,32,128]{2,1,0:T(8,128)S(1)} async-done(((f32[32,32,128]{2,1,0:T(8,128)}), f32[32,32,128]{2,1,0:T(8,128)S(1)}, u32[]{:S(2)}, u32[]{:S(2)}) %all-to-all-start.3) | async-done | bytes 524320 | tf_op jit(solution)/shard_map/while/body/eval_jaxpr/all_to_all | solution.py:17
  183.1 7.1 %all-to-all-done.4 = f32[32,1,1024]{2,1,0:T(1,128)S(1)} async-done(((f32[32,1,1024]{2,1,0:T(1,128)}), f32[32,1,1024]{2,1,0:T(1,128)S(1)}, u32[]{:S(2)}, u32[]{:S(2)}) %all-to-all-start.4) | async-done | bytes 131104 | tf_op jit(solution)/shard_map/while/body/eval_jaxpr/all_to_all | solution.py:17
  201.3 3.9 %all-to-all-start = ((bf16[32,32,1,256]{3,1,2,0:T(8,128)(2,1)}), bf16[32,32,1,256]{3,1,2,0:T(8,128)(2,1)S(1)}, u32[]{:S(2)}, u32[]{:S(2)}) async-start(bf16[32,32,1,256]{3,1,2,0:T(8,128)(2,1)} %broadcast_in_dim.179), calls=%async_computation | async-start | bytes 1048576 | tf_op jit(solution)/shard_map/while/body/eval_jaxpr/all_to_all | solution.py:17
  211.8 5.0 %all-to-all-done = bf16[32,32,1,256]{3,1,2,0:T(8,128)(2,1)S(1)} async-done(((bf16[32,32,1,256]{3,1,2,0:T(8,128)(2,1)}), bf16[32,32,1,256]{3,1,2,0:T(8,128)(2,1)S(1)}, u32[]{:S(2)}, u32[]{:S(2)}) %all-to-all-start) | async-done | bytes 524320 | tf_op jit(solution)/shard_map/while/body/eval_jaxpr/all_to_all | solution.py:17
  225.3 6.9 %all-to-all-done.1 = bf16[32,32,1,256]{3,1,2,0:T(8,128)(2,1)S(1)} async-done(((bf16[32,32,1,256]{3,1,2,0:T(8,128)(2,1)}), bf16[32,32,1,256]{3,1,2,0:T(8,128)(2,1)S(1)}, u32[]{:S(2)}, u32[]{:S(2)}) %all-to-all-start.1) | async-done | bytes 524320 | tf_op jit(solution)/shard_map/while/body/eval_jaxpr/all_to_all | solution.py:33
  232.4 11.6 %all_to_all.75 = f32[4,32,4,256]{3,1,2,0:T(8,128)S(1)} all-to-all(f32[4,32,4,256]{3,1,2,0:T(8,128)S(1)} %broadcast_in_dim.180), channel_id=1, replica_groups=mesh['grp'=4,'row'=32] {'grp'}, dimensions={0} | all-to-all | bytes 1048576 | tf_op jit(solution)/shard_map/while/body/eval_jaxpr/all_to_all | solution.py:17
  245.5 4.8 %all-to-all-start.3 = ((f32[32,32,128]{2,1,0:T(8,128)}), f32[32,32,128]{2,1,0:T(8,128)S(1)}, u32[]{:S(2)}, u32[]{:S(2)}) async-start(f32[32,32,128]{2,1,0:T(8,128)} %broadcast_in_dim.181), calls=%async_computation.3 | async-start | bytes 1048576 | tf_op jit(solution)/shard_map/while/body/eval_jaxpr/all_to_all | solution.py:17
  250.3 11.5 %all-to-all-done.3 = f32[32,32,128]{2,1,0:T(8,128)S(1)} async-done(((f32[32,32,128]{2,1,0:T(8,128)}), f32[32,32,128]{2,1,0:T(8,128)S(1)}, u32[]{:S(2)}, u32[]{:S(2)}) %all-to-all-start.3) | async-done | bytes 524320 | tf_op jit(solution)/shard_map/while/body/eval_jaxpr/all_to_all | solution.py:17
  268.1 7.1 %all-to-all-done.4 = f32[32,1,1024]{2,1,0:T(1,128)S(1)} async-done(((f32[32,1,1024]{2,1,0:T(1,128)}), f32[32,1,1024]{2,1,0:T(1,128)S(1)}, u32[]{:S(2)}, u32[]{:S(2)}) %all-to-all-start.4) | async-done | bytes 131104 | tf_op jit(solution)/shard_map/while/body/eval_jaxpr/all_to_all | solution.py:17
  286.2 3.9 %all-to-all-start = ((bf16[32,32,1,256]{3,1,2,0:T(8,128)(2,1)}), bf16[32,32,1,256]{3,1,2,0:T(8,128)(2,1)S(1)}, u32[]{:S(2)}, u32[]{:S(2)}) async-start(bf16[32,32,1,256]{3,1,2,0:T(8,128)(2,1)} %broadcast_in_dim.179), calls=%async_computation | async-start | bytes 1048576 | tf_op jit(solution)/shard_map/while/body/eval_jaxpr/all_to_all | solution.py:17
  296.7 5.0 %all-to-all-done = bf16[32,32,1,256]{3,1,2,0:T(8,128)(2,1)S(1)} async-done(((bf16[32,32,1,256]{3,1,2,0:T(8,128)(2,1)}), bf16[32,32,1,256]{3,1,2,0:T(8,128)(2,1)S(1)}, u32[]{:S(2)}, u32[]{:S(2)}) %all-to-all-start) | async-done | bytes 524320 | tf_op jit(solution)/shard_map/while/body/eval_jaxpr/all_to_all | solution.py:17
  310.3 6.9 %all-to-all-done.1 = bf16[32,32,1,256]{3,1,2,0:T(8,128)(2,1)S(1)} async-done(((bf16[32,32,1,256]{3,1,2,0:T(8,128)(2,1)}), bf16[32,32,1,256]{3,1,2,0:T(8,128)(2,1)S(1)}, u32[]{:S(2)}, u32[]{:S(2)}) %all-to-all-start.1) | async-done | bytes 524320 | tf_op jit(solution)/shard_map/while/body/eval_jaxpr/all_to_all | solution.py:33
  317.4 11.6 %all_to_all.75 = f32[4,32,4,256]{3,1,2,0:T(8,128)S(1)} all-to-all(f32[4,32,4,256]{3,1,2,0:T(8,128)S(1)} %broadcast_in_dim.180), channel_id=1, replica_groups=mesh['grp'=4,'row'=32] {'grp'}, dimensions={0} | all-to-all | bytes 1048576 | tf_op jit(solution)/shard_map/while/body/eval_jaxpr/all_to_all | solution.py:17
  330.5 4.8 %all-to-all-start.3 = ((f32[32,32,128]{2,1,0:T(8,128)}), f32[32,32,128]{2,1,0:T(8,128)S(1)}, u32[]{:S(2)}, u32[]{:S(2)}) async-start(f32[32,32,128]{2,1,0:T(8,128)} %broadcast_in_dim.181), calls=%async_computation.3 | async-start | bytes 1048576 | tf_op jit(solution)/shard_map/while/body/eval_jaxpr/all_to_all | solution.py:17
  335.3 11.5 %all-to-all-done.3 = f32[32,32,128]{2,1,0:T(8,128)S(1)} async-done(((f32[32,32,128]{2,1,0:T(8,128)}), f32[32,32,128]{2,1,0:T(8,128)S(1)}, u32[]{:S(2)}, u32[]{:S(2)}) %all-to-all-start.3) | async-done | bytes 524320 | tf_op jit(solution)/shard_map/while/body/eval_jaxpr/all_to_all | solution.py:17
  353.1 7.1 %all-to-all-done.4 = f32[32,1,1024]{2,1,0:T(1,128)S(1)} async-done(((f32[32,1,1024]{2,1,0:T(1,128)}), f32[32,1,1024]{2,1,0:T(1,128)S(1)}, u32[]{:S(2)}, u32[]{:S(2)}) %all-to-all-start.4) | async-done | bytes 131104 | tf_op jit(solution)/shard_map/while/body/eval_jaxpr/all_to_all | solution.py:17
  (246 shorter events, 143.0 us)
Async XLA Ops:
  0.6 0.9 copy-start
  2.8 17.0 %all-to-all-start.5 = ((f32[32,1,1024]{2,1,0:T(1,128)}), f32[32,1,1024]{2,1,0:T(1,128)S(1)}, u32[]{:S(2)}, u32[]{:S(2)}) async-start(f32[32,1,1024]{2,1,0:T(1,128)} %reshape.192), calls=%async_computation.5 | async-start | bytes 262144 | tf_op jit(solution)/shard_map/all_to_all | solution.py:17
  28.7 9.9 %copy-start.3 = (s32[32]{0:T(128)S(1)}, s32[32]{0:T(128)}, u32[]{:S(2)}) copy-start(s32[32]{0:T(128)} %get-tuple-element.487) | copy-start | bytes 388 | tf_op jit(solution)/shard_map/while
  29.7 15.5 %all-to-all-start = ((bf16[32,32,1,256]{3,1,2,0:T(8,128)(2,1)}), bf16[32,32,1,256]{3,1,2,0:T(8,128)(2,1)S(1)}, u32[]{:S(2)}, u32[]{:S(2)}) async-start(bf16[32,32,1,256]{3,1,2,0:T(8,128)(2,1)} %broadcast_in_dim.179), calls=%async_computation | async-start | bytes 1048576 | tf_op jit(solution)/shard_map/while/body/eval_jaxpr/all_to_all | solution.py:17
  39.0 14.2 %copy-start.4 = (s32[32]{0:T(128)S(1)}, s32[32]{0:T(128)}, u32[]{:S(2)}) copy-start(s32[32]{0:T(128)} %get-tuple-element.490) | copy-start | bytes 388 | tf_op jit(solution)/shard_map/while
  45.2 15.5 %all-to-all-start.1 = ((bf16[32,32,1,256]{3,1,2,0:T(8,128)(2,1)}), bf16[32,32,1,256]{3,1,2,0:T(8,128)(2,1)S(1)}, u32[]{:S(2)}, u32[]{:S(2)}) async-start(bf16[32,32,1,256]{3,1,2,0:T(8,128)(2,1)} %copy.79), calls=%async_computation.1 | async-start | bytes 1048576 | tf_op jit(solution)/shard_map/while/body/eval_jaxpr/all_to_all | solution.py:33
  49.7 23.8 %copy-start.2 = (f32[1024]{0:T(1024)S(1)}, f32[1024]{0:T(1024)}, u32[]{:S(2)}) copy-start(f32[1024]{0:T(1024)} %get-tuple-element.491) | copy-start | bytes 12292 | tf_op jit(solution)/shard_map/while
  75.0 16.9 %all-to-all-start.3 = ((f32[32,32,128]{2,1,0:T(8,128)}), f32[32,32,128]{2,1,0:T(8,128)S(1)}, u32[]{:S(2)}, u32[]{:S(2)}) async-start(f32[32,32,128]{2,1,0:T(8,128)} %broadcast_in_dim.181), calls=%async_computation.3 | async-start | bytes 1048576 | tf_op jit(solution)/shard_map/while/body/eval_jaxpr/all_to_all | solution.py:17
  93.6 11.6 %all-to-all-start.4 = ((f32[32,1,1024]{2,1,0:T(1,128)}), f32[32,1,1024]{2,1,0:T(1,128)S(1)}, u32[]{:S(2)}, u32[]{:S(2)}) async-start(f32[32,1,1024]{2,1,0:T(1,128)} %reshape.206), calls=%async_computation.4 | async-start | bytes 262144 | tf_op jit(solution)/shard_map/while/body/eval_jaxpr/all_to_all | solution.py:17
  115.3 9.9 %copy-start.3 = (s32[32]{0:T(128)S(1)}, s32[32]{0:T(128)}, u32[]{:S(2)}) copy-start(s32[32]{0:T(128)} %get-tuple-element.487) | copy-start | bytes 388 | tf_op jit(solution)/shard_map/while
  116.3 15.5 %all-to-all-start = ((bf16[32,32,1,256]{3,1,2,0:T(8,128)(2,1)}), bf16[32,32,1,256]{3,1,2,0:T(8,128)(2,1)S(1)}, u32[]{:S(2)}, u32[]{:S(2)}) async-start(bf16[32,32,1,256]{3,1,2,0:T(8,128)(2,1)} %broadcast_in_dim.179), calls=%async_computation | async-start | bytes 1048576 | tf_op jit(solution)/shard_map/while/body/eval_jaxpr/all_to_all | solution.py:17
  125.6 14.2 %copy-start.4 = (s32[32]{0:T(128)S(1)}, s32[32]{0:T(128)}, u32[]{:S(2)}) copy-start(s32[32]{0:T(128)} %get-tuple-element.490) | copy-start | bytes 388 | tf_op jit(solution)/shard_map/while
  131.8 15.5 %all-to-all-start.1 = ((bf16[32,32,1,256]{3,1,2,0:T(8,128)(2,1)}), bf16[32,32,1,256]{3,1,2,0:T(8,128)(2,1)S(1)}, u32[]{:S(2)}, u32[]{:S(2)}) async-start(bf16[32,32,1,256]{3,1,2,0:T(8,128)(2,1)} %copy.79), calls=%async_computation.1 | async-start | bytes 1048576 | tf_op jit(solution)/shard_map/while/body/eval_jaxpr/all_to_all | solution.py:33
  136.3 22.8 %copy-start.2 = (f32[1024]{0:T(1024)S(1)}, f32[1024]{0:T(1024)}, u32[]{:S(2)}) copy-start(f32[1024]{0:T(1024)} %get-tuple-element.491) | copy-start | bytes 12292 | tf_op jit(solution)/shard_map/while
  160.5 16.3 %all-to-all-start.3 = ((f32[32,32,128]{2,1,0:T(8,128)}), f32[32,32,128]{2,1,0:T(8,128)S(1)}, u32[]{:S(2)}, u32[]{:S(2)}) async-start(f32[32,32,128]{2,1,0:T(8,128)} %broadcast_in_dim.181), calls=%async_computation.3 | async-start | bytes 1048576 | tf_op jit(solution)/shard_map/while/body/eval_jaxpr/all_to_all | solution.py:17
  178.6 11.6 %all-to-all-start.4 = ((f32[32,1,1024]{2,1,0:T(1,128)}), f32[32,1,1024]{2,1,0:T(1,128)S(1)}, u32[]{:S(2)}, u32[]{:S(2)}) async-start(f32[32,1,1024]{2,1,0:T(1,128)} %reshape.206), calls=%async_computation.4 | async-start | bytes 262144 | tf_op jit(solution)/shard_map/while/body/eval_jaxpr/all_to_all | solution.py:17
  200.3 9.9 %copy-start.3 = (s32[32]{0:T(128)S(1)}, s32[32]{0:T(128)}, u32[]{:S(2)}) copy-start(s32[32]{0:T(128)} %get-tuple-element.487) | copy-start | bytes 388 | tf_op jit(solution)/shard_map/while
  201.3 15.5 %all-to-all-start = ((bf16[32,32,1,256]{3,1,2,0:T(8,128)(2,1)}), bf16[32,32,1,256]{3,1,2,0:T(8,128)(2,1)S(1)}, u32[]{:S(2)}, u32[]{:S(2)}) async-start(bf16[32,32,1,256]{3,1,2,0:T(8,128)(2,1)} %broadcast_in_dim.179), calls=%async_computation | async-start | bytes 1048576 | tf_op jit(solution)/shard_map/while/body/eval_jaxpr/all_to_all | solution.py:17
  210.6 14.2 %copy-start.4 = (s32[32]{0:T(128)S(1)}, s32[32]{0:T(128)}, u32[]{:S(2)}) copy-start(s32[32]{0:T(128)} %get-tuple-element.490) | copy-start | bytes 388 | tf_op jit(solution)/shard_map/while
  216.8 15.5 %all-to-all-start.1 = ((bf16[32,32,1,256]{3,1,2,0:T(8,128)(2,1)}), bf16[32,32,1,256]{3,1,2,0:T(8,128)(2,1)S(1)}, u32[]{:S(2)}, u32[]{:S(2)}) async-start(bf16[32,32,1,256]{3,1,2,0:T(8,128)(2,1)} %copy.79), calls=%async_computation.1 | async-start | bytes 1048576 | tf_op jit(solution)/shard_map/while/body/eval_jaxpr/all_to_all | solution.py:33
  221.3 22.8 %copy-start.2 = (f32[1024]{0:T(1024)S(1)}, f32[1024]{0:T(1024)}, u32[]{:S(2)}) copy-start(f32[1024]{0:T(1024)} %get-tuple-element.491) | copy-start | bytes 12292 | tf_op jit(solution)/shard_map/while
  245.5 16.3 %all-to-all-start.3 = ((f32[32,32,128]{2,1,0:T(8,128)}), f32[32,32,128]{2,1,0:T(8,128)S(1)}, u32[]{:S(2)}, u32[]{:S(2)}) async-start(f32[32,32,128]{2,1,0:T(8,128)} %broadcast_in_dim.181), calls=%async_computation.3 | async-start | bytes 1048576 | tf_op jit(solution)/shard_map/while/body/eval_jaxpr/all_to_all | solution.py:17
  263.6 11.6 %all-to-all-start.4 = ((f32[32,1,1024]{2,1,0:T(1,128)}), f32[32,1,1024]{2,1,0:T(1,128)S(1)}, u32[]{:S(2)}, u32[]{:S(2)}) async-start(f32[32,1,1024]{2,1,0:T(1,128)} %reshape.206), calls=%async_computation.4 | async-start | bytes 262144 | tf_op jit(solution)/shard_map/while/body/eval_jaxpr/all_to_all | solution.py:17
  285.3 9.9 %copy-start.3 = (s32[32]{0:T(128)S(1)}, s32[32]{0:T(128)}, u32[]{:S(2)}) copy-start(s32[32]{0:T(128)} %get-tuple-element.487) | copy-start | bytes 388 | tf_op jit(solution)/shard_map/while
  286.2 15.5 %all-to-all-start = ((bf16[32,32,1,256]{3,1,2,0:T(8,128)(2,1)}), bf16[32,32,1,256]{3,1,2,0:T(8,128)(2,1)S(1)}, u32[]{:S(2)}, u32[]{:S(2)}) async-start(bf16[32,32,1,256]{3,1,2,0:T(8,128)(2,1)} %broadcast_in_dim.179), calls=%async_computation | async-start | bytes 1048576 | tf_op jit(solution)/shard_map/while/body/eval_jaxpr/all_to_all | solution.py:17
  295.6 14.2 %copy-start.4 = (s32[32]{0:T(128)S(1)}, s32[32]{0:T(128)}, u32[]{:S(2)}) copy-start(s32[32]{0:T(128)} %get-tuple-element.490) | copy-start | bytes 388 | tf_op jit(solution)/shard_map/while
  301.7 15.5 %all-to-all-start.1 = ((bf16[32,32,1,256]{3,1,2,0:T(8,128)(2,1)}), bf16[32,32,1,256]{3,1,2,0:T(8,128)(2,1)S(1)}, u32[]{:S(2)}, u32[]{:S(2)}) async-start(bf16[32,32,1,256]{3,1,2,0:T(8,128)(2,1)} %copy.79), calls=%async_computation.1 | async-start | bytes 1048576 | tf_op jit(solution)/shard_map/while/body/eval_jaxpr/all_to_all | solution.py:33
  306.3 22.8 %copy-start.2 = (f32[1024]{0:T(1024)S(1)}, f32[1024]{0:T(1024)}, u32[]{:S(2)}) copy-start(f32[1024]{0:T(1024)} %get-tuple-element.491) | copy-start | bytes 12292 | tf_op jit(solution)/shard_map/while
  330.5 16.3 %all-to-all-start.3 = ((f32[32,32,128]{2,1,0:T(8,128)}), f32[32,32,128]{2,1,0:T(8,128)S(1)}, u32[]{:S(2)}, u32[]{:S(2)}) async-start(f32[32,32,128]{2,1,0:T(8,128)} %broadcast_in_dim.181), calls=%async_computation.3 | async-start | bytes 1048576 | tf_op jit(solution)/shard_map/while/body/eval_jaxpr/all_to_all | solution.py:17
  348.5 11.6 %all-to-all-start.4 = ((f32[32,1,1024]{2,1,0:T(1,128)}), f32[32,1,1024]{2,1,0:T(1,128)S(1)}, u32[]{:S(2)}, u32[]{:S(2)}) async-start(f32[32,1,1024]{2,1,0:T(1,128)} %reshape.206), calls=%async_computation.4 | async-start | bytes 262144 | tf_op jit(solution)/shard_map/while/body/eval_jaxpr/all_to_all | solution.py:17
  370.3 0.7 copy-start.1
where the time goes:
time: 373 us; the launch traced here: 371 us
  waiting for transfers between devices  129 us (35%)
  starting transfers between devices  76.4 us (20%)
  other arithmetic  49.7 us (13%)
  blocking collectives  47.3 us (13%)
  matrix products  36.5 us (10%)
  local copies, waits for them, and re-layouts  29.3 us (8%)
    all_to_all x13, waiting for transfers between devices, copy_for_each(): lax.all_to_all(jnp.broadcast_to(value[None], (size, *value.shape)), axis,...  101 us
    all_to_all x13, starting transfers between devices, copy_for_each(): lax.all_to_all(jnp.broadcast_to(value[None], (size, *value.shape)), axis,...  60.7 us
    all_to_all x4, blocking collectives, copy_for_each(): lax.all_to_all(jnp.broadcast_to(value[None], (size, *value.shape)), axis,...  47.3 us
    all_to_all x4, waiting for transfers between devices, sent_and_summed(): lax.all_to_all(parts, axis, split_axis=0, concat_axis=0, tiled=True)  27.7 us
    another operation x15, other arithmetic, orthonormal(): lower_factor = jnp.linalg.cholesky(gram_matrix)  18 us
    all_to_all x4, starting transfers between devices, sent_and_summed(): lax.all_to_all(parts, axis, split_axis=0, concat_axis=0, tiled=True)  15.7 us
    another operation x10, other arithmetic, orthonormal(): lax.linalg.triangular_solve(lower_factor, block, left_side=True, lower=True)  15.4 us
    dot_general x4, matrix products, partial_of(): jnp.einsum('kbc,brc->kbr', jnp.take(gathered, cols_here, axis=1), matrix,...  14.1 us
  transfers between devices with their start and end apart: 17, of which 17 were waited for; matrix products, arithmetic and copies ran while one was open for 13% of the time, Pallas kernels for 0%

commit v1 on v0

v1 whole, which is shorter than its diff:
```python
import functools

import jax
import jax.numpy as jnp
from jax import lax
from jax.experimental import pallas as pl
from jax.experimental.pallas import tpu as pltpu
from jax.sharding import PartitionSpec as P

MESH = pl.DeviceIdType.MESH
HIGHEST = lax.Precision.HIGHEST
F32 = jnp.float32
BF16 = jnp.bfloat16

ITERS = 4
K = 32
BS = 256
GRP = 4
ROW = 32
CHIPS = ROW // 2
SIDE = 4
TILES = 32
SHIFT = -1.0

FAR_FIRST = sorted(
    [(dz, dx) for dz in range(SIDE) for dx in range(SIDE) if (dz, dx) != (0, 0)],
    key=lambda d: -(min(d[0], SIDE - d[0]) + min(d[1], SIDE - d[1])),
)
SMALL_GROUP = [(dy, dc) for dy in (2, 1, 3, 0) for dc in (1, 0) if (dy, dc) != (0, 0)]


def height(step):
    return 2 * K if step == 0 else K


def dot(left, right, precision=None):
    return lax.dot_general(
        left, right, (((1,), (0,)), ((), ())), precision=precision, preferred_element_type=F32
    )


def dot_t(left, right, precision=None):
    return lax.dot_general(
        left, right, (((1,), (1,)), ((), ())), precision=precision, preferred_element_type=F32
    )


def cholesky(gram):
    row = lax.broadcasted_iota(jnp.int32, (K, K), 0)
    col = lax.broadcasted_iota(jnp.int32, (K, K), 1)
    left = gram
    right = jnp.where(row == col, 1.0, 0.0).astype(F32)
    for k in range(K - 1):
        factor = jnp.broadcast_to(left[:, k : k + 1], (K, K)) / left[k : k + 1, k : k + 1]
        factor = jnp.where(row > k, factor, 0.0)
        left = left - factor * left[k : k + 1, :]
        right = right - factor * right[k : k + 1, :]
    pivots = jnp.sum(jnp.where(row == col, left, 0.0), axis=1, keepdims=True)
    scale = 1.0 / jnp.sqrt(pivots)
    return jnp.where(col >= row, left * scale, 0.0), right * scale


def kernel(
    slot_ref,
    rows_ref,
    cols_ref,
    tiles_hbm,
    start_ref,
    dual_ref,
    proj_ref,
    fact_ref,
    next_ref,
    tiles,
    cols_0,
    cols_1,
    cols_2,
    cols_3,
    cols_4,
    rows_0,
    rows_1,
    rows_2,
    rows_3,
    raw_x,
    raw_y,
    trans,
    products,
    pair_out,
    pair_in,
    back_out,
    back_in,
    own_back,
    direct_out,
    direct_in,
    dots,
    tile_sem,
    cols_send,
    cols_recv,
    relay_send,
    relay_recv,
    rows_send,
    rows_recv,
    raw_send,
    raw_recv,
    dots_send,
    dots_recv,
    pair_send,
    pair_recv,
    back_send,
    back_recv,
    direct_send,
    direct_recv,
):
    cols_x = (cols_0, cols_1, cols_2, cols_3, cols_4)
    rows_x = (rows_0, rows_1, rows_2, rows_3)
    g = lax.axis_index("grp")
    r = lax.axis_index("row")
    core = lax.rem(r, 2)
    chip = lax.div(r, 2)
    z = lax.div(chip, SIDE)
    x = lax.rem(chip, SIDE)
    partner = r + 1 - 2 * core

    def chip_at(dz, dx):
        return lax.rem(z + dz, SIDE) * SIDE + lax.rem(x + dx, SIDE)

    def chip_from(dz, dx):
        return lax.rem(z + SIDE - dz, SIDE) * SIDE + lax.rem(x + SIDE - dx, SIDE)

    def remote(src, dst, send, recv, group, owner):
        return pltpu.make_async_remote_copy(
            src_ref=src,
            dst_ref=dst,
            send_sem=send,
            recv_sem=recv,
            device_id=(group, owner),
            device_id_type=MESH,
        )

    def await_recv(ref, send, recv):
        remote(ref, ref, send, recv, g, partner).wait_recv()

    def await_send(ref, send, recv):
        remote(ref, ref, send, recv, g, partner).wait_send()

    load = pltpu.make_async_copy(tiles_hbm, tiles, tile_sem)
    load.start()

    barrier = pltpu.get_barrier_semaphore()
    for dz, dx in FAR_FIRST:
        pl.semaphore_signal(
            barrier, inc=1, device_id=(g, chip_at(dz, dx) * 2 + core), device_id_type=MESH
        )
    for dy, dc in SMALL_GROUP:
        pl.semaphore_signal(
            barrier,
            inc=1,
            device_id=(lax.rem(g + dy, GRP), partner if dc else r),
            device_id_type=MESH,
        )

    for i in range(GRP):
        block = start_ref[:, i * BS : (i + 1) * BS]
        high = block.astype(BF16)
        rows_0[i, 0:K, :] = high
        rows_0[i, K : 2 * K, :] = (block - high.astype(F32)).astype(BF16)
        raw_x[i, 0:K, :] = block
    cols_0[r] = rows_0[g]
    trans[...] = jnp.zeros_like(trans)
    products[TILES] = jnp.zeros((K, BS), F32)
    proj_ref[...] = jnp.zeros_like(proj_ref)
    dual = dual_ref[:, pl.ds(pl.multiple_of(g * BS, BS), BS)]

    def send_cols(step):
        here = cols_x[step].at[r]
        for m, (dz, dx) in enumerate(FAR_FIRST):
            remote(
                here, here, cols_send.at[step], cols_recv.at[step, m], g, chip_at(dz, dx) * 2 + core
            ).start()
        if step < ITERS:
            remote(here, here, relay_send.at[step], relay_recv.at[step], g, partner).start()

    def receive_cols(step):
        for m in reversed(range(len(FAR_FIRST))):
            source = chip_from(*FAR_FIRST[m]) * 2 + core
            there = cols_x[step].at[source]
            await_recv(there, cols_send.at[step], cols_recv.at[step, m])
            if step < ITERS:
                remote(there, there, relay_send.at[step], relay_recv.at[step], g, partner).start()

    def products_of(load_left, rows, transposed):
        def body(k, carry):
            tile = tiles[k]
            product = dot_t(load_left(k), tile) if transposed else dot(load_left(k), tile)
            if rows == 2 * K:
                product = product[:K] + product[K:]
            products[k] = product
            return carry

        lax.fori_loop(0, TILES, body, 0, unroll=8)

    def back_sum(owner):
        total = products[slot_ref[owner]]
        for i in range(1, GRP):
            total = total + products[slot_ref[i * ROW + owner]]
        return total

    def send_pairs(step):
        def other(m, carry):
            pair_out[step, m] = back_sum(m * 2 + 1 - core).astype(BF16)
            return carry

        lax.fori_loop(0, CHIPS, other, 0, unroll=2)
        remote(
            pair_out.at[step],
            pair_in.at[step],
            pair_send.at[step],
            pair_recv.at[step],
            g,
            partner,
        ).start()

    def send_back(step):
        def mine(m, carry):
            own_back[m] = back_sum(m * 2 + core)
            return carry

        lax.fori_loop(0, CHIPS, mine, 0, unroll=2)
        await_recv(pair_in.at[step], pair_send.at[step], pair_recv.at[step])
        for dz, dx in FAR_FIRST:
            there = chip_at(dz, dx)
            back_out[step, there] = (
                own_back[there] + pair_in[step, there].astype(F32)
            ).astype(BF16)
        for dz, dx in FAR_FIRST:
            there = chip_at(dz, dx)
            remote(
                back_out.at[step, there],
                back_in.at[step, chip],
                back_send.at[step],
                back_recv.at[step],
                g,
                there * 2 + core,
            ).start()

    def send_direct(step):
        for i in range(GRP):

            def add(j, total, i=i):
                return total + products[slot_ref[i * ROW + j]]

            direct_out[step, i] = lax.fori_loop(
                0, ROW, add, jnp.zeros((K, BS), F32), unroll=8
            )
        for dy in (2, 1, 3):
            group = lax.rem(g + dy, GRP)
            remote(
                direct_out.at[step, group],
                direct_in.at[step, g],
                direct_send.at[step],
                direct_recv.at[step],
                group,
                r,
            ).start()

    def send_dots(step):
        size = height(step)
        width = K * step + 2 * K if step else 2 * K

        def add(p, total):
            owner = p * 2 + core
            so_far = jnp.concatenate([cols_x[s][owner] for s in range(step + 1)], axis=0)
            return total + dot_t(cols_x[step][owner], so_far)

        total = lax.fori_loop(0, CHIPS, add, jnp.zeros((size, width), F32), unroll=4)
        here = g * 2 + core
        if step == 0:
            dots[0, here, :, 0:K] = (total[:K, :K] + total[:K, K:]) + (
                total[K:, :K] + total[K:, K:]
            )
        else:
            dots[step, here, :, 0:K] = total[:, 0:K] + total[:, K : 2 * K]
            dots[step, here, :, K : K + K * step] = total[:, 2 * K :]
        lanes = 128 if step < ITERS else 256
        mine = dots.at[step, here, :, pl.ds(0, lanes)]
        for dy, dc in SMALL_GROUP:
            remote(
                mine,
                mine,
                dots_send.at[step],
                dots_recv.at[step],
                lax.rem(g + dy, GRP),
                partner if dc else r,
            ).start()

    def receive_dots(step):
        lanes = 128 if step < ITERS else 256
        await_recv(
            dots.at[step, pl.ds(0, 7), :, pl.ds(0, lanes)], dots_send.at[step], dots_recv.at[step]
        )
        total = dots[step, 0, :, 0 : K + K * step]
        for i in range(1, 2 * GRP):
            total = total + dots[step, i, :, 0 : K + K * step]
        gram = total[:, K * step :]
        if step > 0:
            before = trans[0 : K * step, 0 : K * step]
            coef = dot_t(total[:, : K * step], before, HIGHEST)
            gram = gram - dot_t(coef, coef, HIGHEST)
        upper, inverse = cholesky(gram)
        trans[K * step : K * step + K, K * step : K * step + K] = inverse
        if step > 0:
            trans[K * step : K * step + K, 0 : K * step] = -dot(
                inverse, dot(coef, before, HIGHEST), HIGHEST
            )
            fact_ref[step - 1] = upper.T
        return coef if step > 0 else None, upper, inverse

    def record(step, coef, upper_before):
        row = lax.broadcasted_iota(jnp.int32, (K, K), 0)
        col = lax.broadcasted_iota(jnp.int32, (K, K), 1)
        at = K * (step - 1)
        if step > 1:
            proj_ref[step - 1, :, 0:at] = coef[:, :at]
            proj_ref[step - 1, :, at - K : at] = coef[:, at - K : at] + upper_before
        proj_ref[step - 1, :, at : at + K] = coef[:, at:] + jnp.where(row == col, SHIFT, 0.0)

    upper_before = None
    for step in range(ITERS):
        size = height(step)
        if step == 0:
            load.wait()
            products_of(lambda k: rows_0[rows_ref[k]], size, False)
            pl.semaphore_wait(barrier, len(FAR_FIRST) + len(SMALL_GROUP))
            send_cols(0)
            send_pairs(0)
        else:
            await_recv(rows_x[step].at[pl.ds(0, 3)], rows_send.at[step], rows_recv.at[step])
            products_of(lambda k, step=step: rows_x[step][rows_ref[k]], size, False)
            send_pairs(step)
        send_back(step)

        receive_cols(step)
        send_dots(step)
        await_recv(cols_x[step].at[pl.ds(0, CHIPS)], relay_send.at[step], relay_recv.at[step])
        products_of(lambda k, step=step: cols_x[step][cols_ref[k]], size, True)
        send_direct(step)

        coef, upper, inverse = receive_dots(step)
        if step > 0:
            record(step, coef, upper_before)
        here = trans[K * step : K * step + K, 0 : K + K * step]
        known = dot(here, raw_x[g, 0 : K + K * step, :], HIGHEST) * (-SHIFT)
        if step > 0:
            older = dot(
                trans[K * (step - 1) : K * step, 0 : K * step], raw_x[g, 0 : K * step, :], HIGHEST
            )
            known = known - dot(upper, older, HIGHEST)
            known = known + dot(here[:, : K * step], raw_y[0 : K * step, :], HIGHEST)
        upper_before = upper

        await_recv(
            direct_in.at[step, pl.ds(0, 3)], direct_send.at[step], direct_recv.at[step]
        )
        total = direct_out[step, g]
        for dy in (1, 2, 3):
            total = total + direct_in[step, lax.rem(g + dy, GRP)]
        await_recv(back_in.at[step, pl.ds(0, CHIPS - 1)], back_send.at[step], back_recv.at[step])
        total = total + own_back[chip] + pair_in[step, chip].astype(F32)
        for dz, dx in FAR_FIRST:
            total = total + back_in[step, chip_at(dz, dx)].astype(F32)
        image = 0.5 * total - raw_x[g, K * step : K * step + K, :] * dual
        raw_y[K * step : K * step + K, :] = image
        block = dot(inverse, image, HIGHEST) + known
        rounded = block.astype(BF16)
        after = step + 1
        cols_x[after][r] = rounded
        raw_x[g, K * after : K * after + K, :] = block
        if after < ITERS:
            rows_x[after][g] = rounded
            mine = rows_x[after].at[g]
            for dy in (2, 1, 3):
                remote(
                    mine, mine, rows_send.at[after], rows_recv.at[after], lax.rem(g + dy, GRP), r
                ).start()
        send_cols(after)
        mine = raw_x.at[g, pl.ds(K * after, K), :]
        for dy in (2, 1, 3):
            remote(
                mine, mine, raw_send.at[after], raw_recv.at[after], lax.rem(g + dy, GRP), r
            ).start()

    receive_cols(ITERS)
    send_dots(ITERS)
    coef, upper, inverse = receive_dots(ITERS)
    record(ITERS, coef, upper_before)
    for step in range(1, ITERS + 1):
        await_recv(
            raw_x.at[pl.ds(0, 3), pl.ds(K * step, K), :], raw_send.at[step], raw_recv.at[step]
        )
    final = trans[K * ITERS : K * ITERS + K, :]
    for i in range(GRP):
        next_ref[:, i * BS : (i + 1) * BS] = dot(final, raw_x[i], HIGHEST)

    for step in range(ITERS + 1):
        await_send(cols_x[step].at[pl.ds(0, CHIPS - 1)], cols_send.at[step], cols_recv.at[step, 0])
        lanes = 128 if step < ITERS else 256
        await_send(
            dots.at[step, pl.ds(0, 7), :, pl.ds(0, lanes)], dots_send.at[step], dots_recv.at[step]
        )
        if step > 0:
            await_send(
                raw_x.at[pl.ds(0, 3), pl.ds(K * step, K), :], raw_send.at[step], raw_recv.at[step]
            )
        if step == ITERS:
            continue
        await_send(cols_x[step].at[pl.ds(0, CHIPS)], relay_send.at[step], relay_recv.at[step])
        await_send(pair_out.at[step], pair_send.at[step], pair_recv.at[step])
        await_send(back_in.at[step, pl.ds(0, CHIPS - 1)], back_send.at[step], back_recv.at[step])
        await_send(direct_in.at[step, pl.ds(0, 3)], direct_send.at[step], direct_recv.at[step])
        if step > 0:
            await_send(rows_x[step].at[pl.ds(0, 3)], rows_send.at[step], rows_recv.at[step])


def per_device(tiles, tile_rows, tile_cols, live_tiles, dual_shift, start_block):
    rows = tile_rows[0, 0]
    cols = tile_cols[0, 0]
    number = jnp.arange(TILES, dtype=jnp.int32)
    place = jnp.where(number < live_tiles[0, 0], rows * ROW + cols, -1)
    slot = TILES - jnp.sum(
        jnp.where(
            place[None, :] == jnp.arange(GRP * ROW, dtype=jnp.int32)[:, None],
            TILES - number[None, :],
            0,
        ),
        axis=1,
    )
    smem = pl.BlockSpec(memory_space=pltpu.SMEM)
    vmem = pl.BlockSpec(memory_space=pltpu.VMEM)
    dma = pltpu.SemaphoreType.DMA
    steps = ITERS + 1
    return pl.pallas_call(
        kernel,
        out_shape=(
            jax.ShapeDtypeStruct((ITERS, K, ITERS * K), F32),
            jax.ShapeDtypeStruct((ITERS, K, K), F32),
            jax.ShapeDtypeStruct((K, GRP * BS), F32),
        ),
        in_specs=[smem, smem, smem, pl.BlockSpec(memory_space=pl.ANY), vmem, vmem],
        out_specs=(vmem, vmem, vmem),
        scratch_shapes=[
            pltpu.VMEM((TILES, BS, BS), BF16),
            *[pltpu.VMEM((ROW, height(step), BS), BF16) for step in range(steps)],
            *[pltpu.VMEM((GRP, height(step), BS), BF16) for step in range(ITERS)],
            pltpu.VMEM((GRP, K * steps, BS), F32),
            pltpu.VMEM((K * ITERS, BS), F32),
            pltpu.VMEM((K * steps, K * steps), F32),
            pltpu.VMEM((TILES + 1, K, BS), F32),
            pltpu.VMEM((ITERS, CHIPS, K, BS), BF16),
            pltpu.VMEM((ITERS, CHIPS, K, BS), BF16),
            pltpu.VMEM((ITERS, CHIPS, K, BS), BF16),
            pltpu.VMEM((ITERS, CHIPS, K, BS), BF16),
            pltpu.VMEM((CHIPS, K, BS), F32),
            pltpu.VMEM((ITERS, GRP, K, BS), F32),
            pltpu.VMEM((ITERS, GRP, K, BS), F32),
            pltpu.VMEM((steps, 2 * GRP, K, 256), F32),
            dma,
            dma((steps,)),
            dma((steps, CHIPS - 1)),
            dma((ITERS,)),
            dma((ITERS,)),
            dma((ITERS,)),
            dma((ITERS,)),
            dma((steps,)),
            dma((steps,)),
            dma((steps,)),
            dma((steps,)),
            dma((ITERS,)),
            dma((ITERS,)),
            dma((ITERS,)),
            dma((ITERS,)),
            dma((ITERS,)),
            dma((ITERS,)),
        ],
        compiler_params=pltpu.CompilerParams(
            collective_id=0, has_side_effects=True, vmem_limit_bytes=60 * 1024 * 1024
        ),
        name="lanczos",
    )(
        slot.astype(jnp.int32),
        rows,
        cols,
        tiles.reshape(TILES, BS, BS),
        start_block,
        dual_shift.reshape(1, GRP * BS),
    )


def solution(mesh):
    in_specs = (
        P("grp", "row", None, None, None),
        P("grp", "row", None),
        P("grp", "row", None),
        P("grp", "row"),
        P("row"),
        P(None, "row"),
    )
    out_specs = (P(), P(), P(None, "row"))
    return jax.shard_map(
        per_device, mesh=mesh, in_specs=in_specs, out_specs=out_specs, check_vma=False
    )
```

time: 373 us -> 102 us (0.27)
  waiting for transfers between devices: 129 us -> 0 us
  Pallas kernels: 0 us -> 94.5 us
  starting transfers between devices: 76.4 us -> 0 us
  other arithmetic: 49.7 us -> 1.29 us
  blocking collectives: 47.3 us -> 0 us
  matrix products: 36.5 us -> 0 us
  local copies, waits for them, and re-layouts: 29.3 us -> 4.51 us
    all_to_all x17 -> x0, waiting for transfers between devices: 129 us -> none  [the longest x13 101 us: copy_for_each(): lax.all_to_all(jnp.broadcast_to(value[None], (size, *value.shape)), axis,...]
    pallas_call x0 -> x1, Pallas kernels: none -> 94.5 us  [per_device(): pl.pallas_call(kernel, out_shape=(jax.ShapeDtypeStruct((ITERS, K, ITERS *...]
    all_to_all x17 -> x0, starting transfers between devices: 76.4 us -> none  [the longest x13 60.7 us: copy_for_each(): lax.all_to_all(jnp.broadcast_to(value[None], (size, *value.shape)), axis,...]
    all_to_all x4 -> x0, blocking collectives: 47.3 us -> none  [copy_for_each(): lax.all_to_all(jnp.broadcast_to(value[None], (size, *value.shape)), axis,...]
    dot_general x29 -> x0, matrix products: 34.8 us -> none  [the longest x4 14.1 us: partial_of(): jnp.einsum('kbc,brc->kbr', jnp.take(gathered, cols_here, axis=1), matrix,...]
    another operation x25 -> x0, other arithmetic: 33.4 us -> none  [the longest x15 18 us: orthonormal(): lower_factor = jnp.linalg.cholesky(gram_matrix)]
    broadcast_in_dim x18 -> x0, local copies, waits for them, and re-layouts: 7.26 us -> none  [the longest x17 7.22 us: copy_for_each(): jnp.broadcast_to(value[None], (size, *value.shape))]
    dynamic_update_slice x4 -> x0, other arithmetic: 5.04 us -> none  [lanczos_step(): lax.dynamic_update_index_in_dim(factors, lower_factor, step_index, 0)]
  transfers between devices with their start and end apart: 17 -> 0, of which waited for: 17 -> 0; matrix products, arithmetic and copies ran while one was open for 13% -> 0% of each run, Pallas kernels for 0% -> 0%
where the time goes in v1:
time: 102 us
  Pallas kernels  94.5 us (93%)
  local copies, waits for them, and re-layouts  4.51 us (4%)
  other arithmetic  1.29 us (1%)
  between operations  1.29 us (1%)
    pallas_call x1, Pallas kernels, per_device(): pl.pallas_call(kernel, out_shape=(jax.ShapeDtypeStruct((ITERS, K, ITERS *...  94.5 us
    unnamed x3, local copies, waits for them, and re-layouts  4.51 us

profile of v1, /device:TPU:1, one launch (start us, length us, event | category | flops | bytes accessed | tf_op | source)
XLA Modules:
  0.0 101.6 jit_solution(4451051190525784000)
XLA Ops:
  1.3 0.7 compare_select_fusion
  2.0 0.1 select_reduce_fusion
  2.0 0.5 broadcast_subtract_fusion.slot_ref
  2.6 94.5 %lanczos.1 = (f32[4,32,128]{2,1,0:T(8,128)}, f32[4,32,32]{2,1,0:T(8,128)}, f32[32,1024]{1,0:T(8,128)}) custom-call(s32[128]{0:T(128)} %broadcast_subtract_fusion.slot_ref, s32[32]{0:T(128)} %bitcast.11, s32[32]{0:T(128)} %bitcast.10, bf16[32,256,256]{2,1,0:T(8,128)(2,1)} %bitcast.8, f32[32,1024]{1,0:T(8,128)} %start_ref.1, f32[1,1024]{1,0:T(1,128)} %bitcast.9), custom_call_target="tpu_custom_call" | custom-call | tf_op jit(solution)/shard_map/lanczos/pallas_call | solution.py:440
  97.1 1.5 %copy.13 = f32[4,32,128]{2,1,0:T(8,128)} copy(f32[4,32,128]{2,1,0:T(8,128)} %get-tuple-element.8) | data formatting | bytes 131072
  98.5 1.5 %copy.14 = f32[4,32,32]{2,1,0:T(8,128)} copy(f32[4,32,32]{2,1,0:T(8,128)} %get-tuple-element.9) | data formatting | bytes 32768
  100.0 1.6 %copy.15 = f32[32,1024]{1,0:T(8,128)} copy(f32[32,1024]{1,0:T(8,128)} %get-tuple-element.10) | data formatting | bytes 262144

commit v2 on v1

v2 whole, which is shorter than its diff:
```python
import functools

import jax
import jax.numpy as jnp
from jax import lax
from jax.experimental import pallas as pl
from jax.experimental.pallas import tpu as pltpu
from jax.sharding import PartitionSpec as P

MESH = pl.DeviceIdType.MESH
HIGHEST = lax.Precision.HIGHEST
F32 = jnp.float32
BF16 = jnp.bfloat16

ITERS = 4
K = 32
BS = 256
GRP = 4
ROW = 32
CHIPS = ROW // 2
SIDE = 4
TILES = 32
SHIFT = -1.0

FAR_FIRST = sorted(
    [(dz, dx) for dz in range(SIDE) for dx in range(SIDE) if (dz, dx) != (0, 0)],
    key=lambda d: -(min(d[0], SIDE - d[0]) + min(d[1], SIDE - d[1])),
)
SMALL_GROUP = [(dy, dc) for dy in (2, 1, 3, 0) for dc in (1, 0) if (dy, dc) != (0, 0)]


def height(step):
    return 2 * K if step == 0 else K


def dots_height(step):
    return K if step < ITERS else K + 8


def dot(left, right, precision=None):
    return lax.dot_general(
        left, right, (((1,), (0,)), ((), ())), precision=precision, preferred_element_type=F32
    )


def dot_t(left, right, precision=None):
    return lax.dot_general(
        left, right, (((1,), (1,)), ((), ())), precision=precision, preferred_element_type=F32
    )


def cholesky(gram):
    row = lax.broadcasted_iota(jnp.int32, (K, K), 0)
    col = lax.broadcasted_iota(jnp.int32, (K, K), 1)
    left = gram
    right = jnp.where(row == col, 1.0, 0.0).astype(F32)
    for k in range(0, K - 2, 2):
        first = jnp.broadcast_to(left[:, k : k + 1], (K, K))
        second = jnp.broadcast_to(left[:, k + 1 : k + 2], (K, K))
        a = first[k : k + 1, :]
        b = second[k : k + 1, :]
        d = second[k + 1 : k + 2, :]
        inverse = 1.0 / (a * d - b * b)
        below = row > k + 1
        of_first = jnp.where(below, first * (d * inverse) - second * (b * inverse), 0.0)
        of_second = jnp.where(below, second * (a * inverse) - first * (b * inverse), 0.0)
        left_k, left_l = left[k : k + 1, :], left[k + 1 : k + 2, :]
        right_k, right_l = right[k : k + 1, :], right[k + 1 : k + 2, :]
        left = left - of_first * left_k - of_second * left_l
        right = right - of_first * right_k - of_second * right_l
    odd = (row & 1) == 1
    pivots = jnp.sum(jnp.where(row == col, left, 0.0), axis=1, keepdims=True)
    beside = jnp.sum(jnp.where(row + 1 == col, left, 0.0), axis=1, keepdims=True)
    factor = jnp.where(odd, pltpu.roll(jnp.broadcast_to(beside / pivots, (K, K)), 1, 0), 0.0)
    left = left - factor * pltpu.roll(left, 1, 0)
    right = right - factor * pltpu.roll(right, 1, 0)
    pivots = jnp.sum(jnp.where(row == col, left, 0.0), axis=1, keepdims=True)
    scale = 1.0 / jnp.sqrt(pivots)
    return jnp.where(col >= row, left * scale, 0.0), jnp.where(col <= row, right * scale, 0.0)


def kernel(
    rows_hbm,
    cols_hbm,
    live_hbm,
    tiles_hbm,
    start_hbm,
    dual_hbm,
    proj_hbm,
    fact_hbm,
    next_hbm,
    rows_smem,
    cols_smem,
    live_smem,
    dual_ref,
    proj_ref,
    fact_ref,
    next_ref,
    gram_ref,
    start_gram,
    start_grams,
    slot_vmem,
    slot_ref,
    start_ref,
    tiles,
    cols_0,
    cols_1,
    cols_2,
    cols_3,
    cols_4,
    rows_0,
    rows_1,
    rows_2,
    rows_3,
    raw_x,
    basis,
    trans,
    products,
    pair_out,
    pair_in,
    back_out,
    back_in,
    own_back,
    own_direct,
    direct_out,
    direct_in,
    dots,
    load_sem,
    store_sem,
    slot_sem,
    tile_sem,
    pair_gram_send,
    pair_gram_recv,
    gram_send,
    gram_recv,
    cols_send,
    cols_recv,
    relay_send,
    relay_recv,
    rows_send,
    rows_recv,
    raw_send,
    raw_recv,
    dots_send,
    dots_recv,
    pair_send,
    pair_recv,
    back_send,
    back_recv,
    direct_send,
    direct_recv,
):
    cols_x = (cols_0, cols_1, cols_2, cols_3, cols_4)
    rows_x = (rows_0, rows_1, rows_2, rows_3)
    g = lax.axis_index("grp")
    r = lax.axis_index("row")
    core = lax.rem(r, 2)
    chip = lax.div(r, 2)
    z = lax.div(chip, SIDE)
    x = lax.rem(chip, SIDE)
    partner = r + 1 - 2 * core

    def chip_at(dz, dx):
        return lax.rem(z + dz, SIDE) * SIDE + lax.rem(x + dx, SIDE)

    def chip_from(dz, dx):
        return lax.rem(z + SIDE - dz, SIDE) * SIDE + lax.rem(x + SIDE - dx, SIDE)

    def remote(src, dst, send, recv, group, owner):
        return pltpu.make_async_remote_copy(
            src_ref=src,
            dst_ref=dst,
            send_sem=send,
            recv_sem=recv,
            device_id=(group, owner),
            device_id_type=MESH,
        )

    def await_recv(ref, send, recv):
        remote(ref, ref, send, recv, g, partner).wait_recv()

    def await_send(ref, send, recv):
        remote(ref, ref, send, recv, g, partner).wait_send()

    barrier = pltpu.get_barrier_semaphore()
    for dz, dx in FAR_FIRST:
        pl.semaphore_signal(
            barrier, inc=1, device_id=(g, chip_at(dz, dx) * 2 + core), device_id_type=MESH
        )
    for dy, dc in SMALL_GROUP:
        pl.semaphore_signal(
            barrier,
            inc=1,
            device_id=(lax.rem(g + dy, GRP), partner if dc else r),
            device_id_type=MESH,
        )

    loads = [
        pltpu.make_async_copy(src, dst, load_sem.at[i])
        for i, (src, dst) in enumerate(
            [
                (rows_hbm, rows_smem),
                (cols_hbm, cols_smem),
                (live_hbm, live_smem),
                (start_hbm, start_ref),
                (dual_hbm, dual_ref),
            ]
        )
    ]
    for copy in loads:
        copy.start()
    load = pltpu.make_async_copy(tiles_hbm, tiles, tile_sem)
    load.start()

    trans[...] = jnp.zeros_like(trans)
    products[TILES] = jnp.zeros((K, BS), F32)
    proj_ref[...] = jnp.zeros_like(proj_ref)
    for copy in loads:
        copy.wait()

    lane = lax.broadcasted_iota(jnp.int32, (1, GRP * ROW), 1)
    slots = jnp.full((1, GRP * ROW), TILES, jnp.int32)
    for k in range(TILES):
        place = jnp.where(live_smem[0, 0] > k, rows_smem[0, 0, k] * ROW + cols_smem[0, 0, k], -1)
        slots = jnp.where(lane == place, k, slots)
    slot_vmem[...] = slots
    table = pltpu.make_async_copy(slot_vmem, slot_ref, slot_sem)
    table.start()

    for i in range(GRP):
        block = start_ref[:, i * BS : (i + 1) * BS]
        high = block.astype(BF16)
        rows_0[i, 0:K, :] = high
        rows_0[i, K : 2 * K, :] = (block - high.astype(F32)).astype(BF16)
        raw_x[i, 0:K, :] = block
    cols_0[r] = rows_0[g]
    gram = dot_t(start_ref[...], start_ref[...], HIGHEST)
    for i in range(4):
        start_gram[core, :, i * K : (i + 1) * K] = gram[8 * i : 8 * i + 8]
    dual = dual_ref[:, pl.ds(pl.multiple_of(g * BS, BS), BS)]

    def send_cols(step):
        here = cols_x[step].at[r]
        for m, (dz, dx) in enumerate(FAR_FIRST):
            remote(
                here, here, cols_send.at[step], cols_recv.at[step, m], g, chip_at(dz, dx) * 2 + core
            ).start()
        if step < ITERS:
            remote(here, here, relay_send.at[step], relay_recv.at[step], g, partner).start()

    def receive_cols(step):
        for m in reversed(range(len(FAR_FIRST))):
            source = chip_from(*FAR_FIRST[m]) * 2 + core
            there = cols_x[step].at[source]
            await_recv(there, cols_send.at[step], cols_recv.at[step, m])
            if step < ITERS:
                remote(there, there, relay_send.at[step], relay_recv.at[step], g, partner).start()

    def products_of(load_left, rows, transposed):
        def body(k, carry):
            tile = tiles[k]
            product = dot_t(load_left(k), tile) if transposed else dot(load_left(k), tile)
            if rows == 2 * K:
                product = product[:K] + product[K:]
            products[k] = product
            return carry

        lax.fori_loop(0, TILES, body, 0, unroll=True)

    def back_sum(owner):
        total = products[slot_ref[0, owner]]
        for i in range(1, GRP):
            total = total + products[slot_ref[0, i * ROW + owner]]
        return total

    def send_pairs(step):
        def other(m, carry):
            pair_out[step, m] = back_sum(m * 2 + 1 - core).astype(BF16)
            return carry

        lax.fori_loop(0, CHIPS, other, 0, unroll=2)
        remote(
            pair_out.at[step],
            pair_in.at[step],
            pair_send.at[step],
            pair_recv.at[step],
            g,
            partner,
        ).start()

    def own_sums(step):
        def mine(m, carry):
            own_back[m] = back_sum(m * 2 + core)
            return carry

        lax.fori_loop(0, CHIPS, mine, 0, unroll=2)

    def send_back(step):
        with jax.named_scope("wait_pair"):
            await_recv(pair_in.at[step], pair_send.at[step], pair_recv.at[step])
        for dz, dx in FAR_FIRST:
            there = chip_at(dz, dx)
            back_out[step, there] = (
                own_back[there] + pair_in[step, there].astype(F32)
            ).astype(BF16)
        for dz, dx in FAR_FIRST:
            there = chip_at(dz, dx)
            remote(
                back_out.at[step, there],
                back_in.at[step, chip],
                back_send.at[step],
                back_recv.at[step],
                g,
                there * 2 + core,
            ).start()

    def send_direct(step):
        for dy in (2, 1, 3, 0):
            group = lax.rem(g + dy, GRP)

            def add(j, total, group=group):
                return total + products[slot_ref[0, group * ROW + j]]

            total = lax.fori_loop(0, ROW, add, jnp.zeros((K, BS), F32), unroll=8)
            if dy == 0:
                own_direct[...] = total
                continue
            direct_out[step, group] = total.astype(BF16)
            remote(
                direct_out.at[step, group],
                direct_in.at[step, g],
                direct_send.at[step],
                direct_recv.at[step],
                group,
                r,
            ).start()

    def send_start_gram():
        await_recv(start_gram.at[0], pair_gram_send, pair_gram_recv)
        start_grams[chip] = start_gram[0] + start_gram[1]
        mine = start_grams.at[chip]
        for dz, dx in FAR_FIRST:
            remote(mine, mine, gram_send, gram_recv, g, chip_at(dz, dx) * 2 + core).start()

    def receive_start_gram():
        await_recv(start_grams.at[pl.ds(0, CHIPS - 1)], gram_send, gram_recv)
        total = start_grams[0]
        for i in range(1, CHIPS):
            total = total + start_grams[i]
        return jnp.concatenate([total[:, i * K : (i + 1) * K] for i in range(4)], axis=0)

    def send_dots(step):
        width = K * step + 2 * K

        def add(p, total):
            owner = p * 2 + core
            so_far = jnp.concatenate([cols_x[s][owner] for s in range(step + 1)], axis=0)
            return total + dot_t(cols_x[step][owner], so_far)

        total = lax.fori_loop(0, CHIPS, add, jnp.zeros((K, width), F32), unroll=True)
        here = g * 2 + core
        dots[step, here, 0:K, 0:K] = total[:, 0:K] + total[:, K : 2 * K]
        if step > 1:
            dots[step, here, 0:K, K : K * step] = total[:, 2 * K : K + K * step]
        gram = total[:, K + K * step :]
        if step < ITERS:
            dots[step, here, 0:K, K * step : K + K * step] = gram
        else:
            for i in range(4):
                dots[step, here, K:, i * K : (i + 1) * K] = gram[8 * i : 8 * i + 8]
        mine = dots.at[step, here, pl.ds(0, dots_height(step))]
        for dy, dc in SMALL_GROUP:
            remote(
                mine,
                mine,
                dots_send.at[step],
                dots_recv.at[step],
                lax.rem(g + dy, GRP),
                partner if dc else r,
            ).start()

    def receive_dots(step):
        with jax.named_scope("wait_dots"):
            await_recv(
                dots.at[step, pl.ds(0, 7), pl.ds(0, dots_height(step))],
                dots_send.at[step],
                dots_recv.at[step],
            )
        total = dots[step, 0, 0 : dots_height(step)]
        for i in range(1, 2 * GRP):
            total = total + dots[step, i, 0 : dots_height(step)]
        if step < ITERS:
            gram = total[:, K * step : K + K * step]
        else:
            gram = jnp.concatenate([total[K:, i * K : (i + 1) * K] for i in range(4)], axis=0)
        coef = dot_t(total[0:K, : K * step], trans[0 : K * step, 0 : K * step], HIGHEST)
        if step > 1:
            coef = dot(inverses[step - 1], coef, HIGHEST)
            gram = dot_t(dot(inverses[step - 1], gram, HIGHEST), inverses[step - 1], HIGHEST)
        gram_ref[...] = gram - dot_t(coef, coef, HIGHEST)
        return coef, gram_ref[...]

    def normalise(step, coef, gram):
        with jax.named_scope("cholesky"):
            upper, inverse = cholesky(gram)
        own = inverse if step < 2 else dot(inverse, inverses[step - 1], HIGHEST)
        trans[K * step : K + K * step, K * step : K + K * step] = own
        if step > 0:
            fact_ref[step - 1] = upper.T
            trans[K * step : K + K * step, 0 : K * step] = -dot(
                inverse,
                dot(coef, trans[0 : K * step, 0 : K * step], HIGHEST),
                HIGHEST,
            )
        uppers[step] = upper
        inverses[step] = inverse

    def record(step, coef):
        row = lax.broadcasted_iota(jnp.int32, (K, K), 0)
        col = lax.broadcasted_iota(jnp.int32, (K, K), 1)
        at = K * (step - 1)
        if step > 1:
            if step > 2:
                proj_ref[step - 1, :, 0 : at - K] = coef[:, : at - K]
            proj_ref[step - 1, :, at - K : at] = coef[:, at - K : at] + uppers[step - 1]
        proj_ref[step - 1, :, at : at + K] = coef[:, at:] + jnp.where(row == col, SHIFT, 0.0)

    stores = [
        pltpu.make_async_copy(src, dst, store_sem.at[i])
        for i, (src, dst) in enumerate(
            [(proj_ref, proj_hbm), (fact_ref, fact_hbm), (next_ref, next_hbm)]
        )
    ]
    uppers = {}
    inverses = {}
    scope = jax.named_scope
    ahead = None
    for step in range(ITERS):
        size = height(step)
        if ahead is not None:
            ahead()
        if step == 0:
            with scope("load"):
                load.wait()
                table.wait()
            with scope("back"):
                products_of(lambda k: rows_0[rows_smem[0, 0, k]], size, False)
            with scope("enter"):
                pl.semaphore_wait(barrier, len(FAR_FIRST) + len(SMALL_GROUP))
            mine = start_gram.at[core]
            remote(mine, mine, pair_gram_send, pair_gram_recv, g, partner).start()
            send_cols(0)
        else:
            with scope("wait_rows"):
                await_recv(rows_x[step].at[pl.ds(0, 3)], rows_send.at[step], rows_recv.at[step])
            with scope("back"):
                products_of(lambda k, step=step: rows_x[step][rows_smem[0, 0, k]], size, False)
        with scope("pairs"):
            send_pairs(step)
        with scope("own_sums"):
            own_sums(step)
            if step == 0:
                send_start_gram()
        with scope("wait_cols"):
            receive_cols(step)
        with scope("send_back"):
            send_back(step)
        if step > 0:
            with scope("dots"):
                send_dots(step)
        with scope("wait_relay"):
            await_recv(cols_x[step].at[pl.ds(0, CHIPS)], relay_send.at[step], relay_recv.at[step])
        with scope("forward"):
            products_of(lambda k, step=step: cols_x[step][cols_smem[0, 0, k]], size, True)
        with scope("direct"):
            send_direct(step)

        if step == 0:
            with scope("wait_dots"):
                coef, gram = None, receive_start_gram()
            normalise(0, None, gram)
            scaled = dot(inverses[0], raw_x[g, 0:K, :], HIGHEST)
            known = scaled * (-SHIFT)
            basis[0:K, 0:BS] = scaled
        else:
            coef, gram = receive_dots(step)
            with scope("known"):
                block = raw_x[g, K * step : K * step + K, :]
                if step > 1:
                    block = dot(inverses[step - 1], block, HIGHEST)
                in_basis = dot(coef, basis[0 : K * step, :], HIGHEST)
                block = block - in_basis[:, :BS]
                known = (
                    block * (-SHIFT)
                    - in_basis[:, BS:]
                    - dot(gram, basis[K * (step - 1) : K * step, 0:BS], HIGHEST)
                )

        with scope("wait_direct"):
            await_recv(
                direct_in.at[step, pl.ds(0, 3)], direct_send.at[step], direct_recv.at[step]
            )
        with scope("wait_back"):
            await_recv(
                back_in.at[step, pl.ds(0, CHIPS - 1)], back_send.at[step], back_recv.at[step]
            )
        with scope("update"):
            total = own_direct[...]
            for dy in (1, 2, 3):
                total = total + direct_in[step, lax.rem(g + dy, GRP)].astype(F32)
            total = total + own_back[chip] + pair_in[step, chip].astype(F32)
            for dz, dx in FAR_FIRST:
                total = total + back_in[step, chip_at(dz, dx)].astype(F32)
            image = 0.5 * total - raw_x[g, K * step : K * step + K, :] * dual
            if step == 0:
                image = dot(inverses[0], image, HIGHEST)
                basis[0:K, BS:] = image
                following = image + known
            else:
                if step > 1:
                    image = dot(inverses[step - 1], image, HIGHEST)
                following = image + known
                image = image - in_basis[:, BS:]
            rounded = following.astype(BF16)
            after = step + 1
            cols_x[after][r] = rounded
            raw_x[g, K * after : K * after + K, :] = following
            if after < ITERS:
                rows_x[after][g] = rounded
                mine = rows_x[after].at[g]
                for dy in (2, 1, 3):
                    remote(
                        mine,
                        mine,
                        rows_send.at[after],
                        rows_recv.at[after],
                        lax.rem(g + dy, GRP),
                        r,
                    ).start()
            send_cols(after)
            mine = raw_x.at[g, pl.ds(K * after, K), :]
            for dy in (2, 1, 3):
                remote(
                    mine, mine, raw_send.at[after], raw_recv.at[after], lax.rem(g + dy, GRP), r
                ).start()

        def ahead(step=step, coef=coef, gram=gram, block=None if step == 0 else block, image=image):
            if step > 0:
                normalise(step, coef, gram)
                at = K * step
                basis[at : at + K, 0:BS] = dot(inverses[step], block, HIGHEST)
                basis[at : at + K, BS:] = dot(inverses[step], image, HIGHEST)
                record(step, coef)

    ahead()
    with scope("wait_cols"):
        receive_cols(ITERS)
    with scope("dots"):
        send_dots(ITERS)
    coef, gram = receive_dots(ITERS)
    normalise(ITERS, coef, gram)
    with scope("final"):
        record(ITERS, coef)
        for step in range(1, ITERS + 1):
            await_recv(
                raw_x.at[pl.ds(0, 3), pl.ds(K * step, K), :], raw_send.at[step], raw_recv.at[step]
            )
        final = trans[K * ITERS : K * ITERS + K, :]
        for copy in stores[:2]:
            copy.start()
        for i in range(GRP):
            next_ref[:, i * BS : (i + 1) * BS] = dot(final, raw_x[i], HIGHEST)

    stores[2].start()
    await_send(start_gram.at[0], pair_gram_send, pair_gram_recv)
    await_send(start_grams.at[pl.ds(0, CHIPS - 1)], gram_send, gram_recv)
    for step in range(ITERS + 1):
        await_send(cols_x[step].at[pl.ds(0, CHIPS - 1)], cols_send.at[step], cols_recv.at[step, 0])
        if step > 0:
            await_send(
                dots.at[step, pl.ds(0, 7), pl.ds(0, dots_height(step))],
                dots_send.at[step],
                dots_recv.at[step],
            )
        if step > 0:
            await_send(
                raw_x.at[pl.ds(0, 3), pl.ds(K * step, K), :], raw_send.at[step], raw_recv.at[step]
            )
        if step == ITERS:
            continue
        await_send(cols_x[step].at[pl.ds(0, CHIPS)], relay_send.at[step], relay_recv.at[step])
        await_send(pair_out.at[step], pair_send.at[step], pair_recv.at[step])
        await_send(back_in.at[step, pl.ds(0, CHIPS - 1)], back_send.at[step], back_recv.at[step])
        await_send(direct_in.at[step, pl.ds(0, 3)], direct_send.at[step], direct_recv.at[step])
        if step > 0:
            await_send(rows_x[step].at[pl.ds(0, 3)], rows_send.at[step], rows_recv.at[step])
    for copy in stores:
        copy.wait()


def write_out(*refs):
    inputs, outputs, held, sems = refs[:3], refs[3:6], refs[6:9], refs[9]
    reads = [pltpu.make_async_copy(inputs[i], held[i], sems.at[0, i]) for i in range(3)]
    writes = [pltpu.make_async_copy(held[i], outputs[i], sems.at[1, i]) for i in range(3)]
    for copy in reads:
        copy.start()
    for i in range(3):
        reads[i].wait()
        writes[i].start()
    for copy in writes:
        copy.wait()


def per_device(tiles, tile_rows, tile_cols, live_tiles, dual_shift, start_block):
    hbm = pl.BlockSpec(memory_space=pltpu.HBM)
    dma = pltpu.SemaphoreType.DMA
    steps = ITERS + 1
    out = pl.pallas_call(
        kernel,
        out_shape=(
            jax.ShapeDtypeStruct((ITERS, K, ITERS * K), F32),
            jax.ShapeDtypeStruct((ITERS, K, K), F32),
            jax.ShapeDtypeStruct((K, GRP * BS), F32),
        ),
        in_specs=[hbm] * 6,
        out_specs=(hbm, hbm, hbm),
        scratch_shapes=[
            pltpu.SMEM((1, 1, TILES), jnp.int32),
            pltpu.SMEM((1, 1, TILES), jnp.int32),
            pltpu.SMEM((1, 1), jnp.int32),
            pltpu.VMEM((1, GRP * BS), F32),
            pltpu.VMEM((ITERS, K, ITERS * K), F32),
            pltpu.VMEM((ITERS, K, K), F32),
            pltpu.VMEM((K, GRP * BS), F32),
            pltpu.VMEM((K, K), F32),
            pltpu.VMEM((2, 8, 128), F32),
            pltpu.VMEM((CHIPS, 8, 128), F32),
            pltpu.VMEM((1, GRP * ROW), jnp.int32),
            pltpu.SMEM((1, GRP * ROW), jnp.int32),
            pltpu.VMEM((K, GRP * BS), F32),
            pltpu.VMEM((TILES, BS, BS), BF16),
            *[pltpu.VMEM((ROW, height(step), BS), BF16) for step in range(steps)],
            *[pltpu.VMEM((GRP, height(step), BS), BF16) for step in range(ITERS)],
            pltpu.VMEM((GRP, K * steps, BS), F32),
            pltpu.VMEM((K * ITERS, 2 * BS), F32),
            pltpu.VMEM((K * steps, K * steps), F32),
            pltpu.VMEM((TILES + 1, K, BS), F32),
            pltpu.VMEM((ITERS, CHIPS, K, BS), BF16),
            pltpu.VMEM((ITERS, CHIPS, K, BS), BF16),
            pltpu.VMEM((ITERS, CHIPS, K, BS), BF16),
            pltpu.VMEM((ITERS, CHIPS, K, BS), BF16),
            pltpu.VMEM((CHIPS, K, BS), F32),
            pltpu.VMEM((K, BS), F32),
            pltpu.VMEM((ITERS, GRP, K, BS), BF16),
            pltpu.VMEM((ITERS, GRP, K, BS), BF16),
            pltpu.VMEM((steps, 2 * GRP, K + 8, 128), F32),
            dma((5,)),
            dma((3,)),
            dma,
            dma,
            dma,
            dma,
            dma,
            dma,
            dma((steps,)),
            dma((steps, CHIPS - 1)),
            dma((ITERS,)),
            dma((ITERS,)),
            dma((ITERS,)),
            dma((ITERS,)),
            dma((steps,)),
            dma((steps,)),
            dma((steps,)),
            dma((steps,)),
            dma((ITERS,)),
            dma((ITERS,)),
            dma((ITERS,)),
            dma((ITERS,)),
            dma((ITERS,)),
            dma((ITERS,)),
        ],
        compiler_params=pltpu.CompilerParams(
            collective_id=0, has_side_effects=True, vmem_limit_bytes=60 * 1024 * 1024
        ),
        name="lanczos",
    )(
        tile_rows,
        tile_cols,
        live_tiles,
        tiles.reshape(TILES, BS, BS),
        start_block,
        dual_shift.reshape(1, GRP * BS),
    )
    return pl.pallas_call(
        write_out,
        out_shape=tuple(jax.ShapeDtypeStruct(a.shape, a.dtype) for a in out),
        in_specs=[hbm] * 3,
        out_specs=(hbm, hbm, hbm),
        scratch_shapes=[*[pltpu.VMEM(a.shape, a.dtype) for a in out], dma((2, 3))],
        compiler_params=pltpu.CompilerParams(vmem_limit_bytes=60 * 1024 * 1024),
        name="write_out",
    )(*out)


def solution(mesh):
    in_specs = (
        P("grp", "row", None, None, None),
        P("grp", "row", None),
        P("grp", "row", None),
        P("grp", "row"),
        P("row"),
        P(None, "row"),
    )
    out_specs = (P(), P(), P(None, "row"))
    return jax.shard_map(
        per_device, mesh=mesh, in_specs=in_specs, out_specs=out_specs, check_vma=False
    )
```

time: 102 us -> 82.3 us (0.81)
  Pallas kernels: 94.5 us -> 80.9 us
  local copies, waits for them, and re-layouts: 4.51 us -> 0 us
  other arithmetic: 1.29 us -> 0 us
    pallas_call x1, Pallas kernels: 94.5 us -> 79.2 us  [per_device(): pl.pallas_call(kernel, out_shape=(jax.ShapeDtypeStruct((ITERS, K, ITERS *...]
    unnamed x3 -> x0, local copies, waits for them, and re-layouts: 4.51 us -> none
    pallas_call x0 -> x1, Pallas kernels: none -> 1.68 us  [per_device(): pl.pallas_call(write_out, out_shape=tuple((jax.ShapeDtypeStruct(a.shape,...]
where the time goes in v2:
time: 82.3 us; the launch traced here: 82.2 us
  Pallas kernels  80.9 us (98%)
  between operations  1.29 us (2%)
    pallas_call x1, Pallas kernels, per_device(): pl.pallas_call(kernel, out_shape=(jax.ShapeDtypeStruct((ITERS, K, ITERS *...  79.2 us
    pallas_call x1, Pallas kernels, per_device(): pl.pallas_call(write_out, out_shape=tuple((jax.ShapeDtypeStruct(a.shape,...  1.68 us

profile of v2, /device:TPU:1, one launch (start us, length us, event | category | flops | bytes accessed | tf_op | source)
XLA Modules:
  0.0 82.2 jit_solution(2157168146153207405)
XLA Ops:
  1.3 79.2 %lanczos.1 = (f32[4,32,128]{2,1,0:T(8,128)}, f32[4,32,32]{2,1,0:T(8,128)}, f32[32,1024]{1,0:T(8,128)}) custom-call(s32[1,1,32]{2,1,0:T(1,128)} %rows_hbm.1, s32[1,1,32]{2,1,0:T(1,128)} %cols_hbm.1, s32[1,1]{1,0:T(1,128)S(6)} %copy.9.live_hbm, bf16[32,256,256]{2,1,0:T(8,128)(2,1)} %bitcast.2, f32[32,1024]{1,0:T(8,128)} %start_hbm.1, f32[1,1024]{1,0:T(1,128)} %bitcast.3), custom_call_target="tpu_custom_call" | custom-call | tf_op jit(solution)/shard_map/lanczos/pallas_call | solution.py:618
  80.5 1.7 %write_out.1 = (f32[4,32,128]{2,1,0:T(8,128)}, f32[4,32,32]{2,1,0:T(8,128)}, f32[32,1024]{1,0:T(8,128)}) custom-call(f32[4,32,128]{2,1,0:T(8,128)} %get-tuple-element.6.refs_0_, f32[4,32,32]{2,1,0:T(8,128)} %get-tuple-element.7.refs_1_, f32[32,1024]{1,0:T(8,128)} %get-tuple-element.8.refs_2_), custom_call_target="tpu_custom_call" | custom-call | tf_op jit(solution)/shard_map/write_out/pallas_call | solution.py:694
